TPU v7x, 512 devices: a whole 4x8x8 slice. The times are simulated.
512 devices in a mesh: rep: 32 (over x, y), shard: 16 (over z, core).
Axes of the slice: x: 4, y: 8, z: 8, core: 2. Of those that a mesh axis runs over, the one named last changes fastest.
Arguments:
- deltas: bfloat16 [32, 2048, 4096], P('rep', 'shard'), may hold values from -6 to 6
- presence: int32 [32], replicated, may hold values from 0 to 1, as said below
- owner_of: int32 [32], replicated, may hold values from 0 to 31, each once
- outer_params: float32 [2048, 4096], P('shard', 'rep'), may hold values from -6 to 6
- momentum: float32 [2048, 4096], P('shard', 'rep'), may hold values from -4 to 4
Outputs:
- new_weights: bfloat16 [2048, 4096], P('shard')
- new_outer: float32 [2048, 4096], P('shard', 'rep')
- new_momentum: float32 [2048, 4096], P('shard', 'rep')
Inputs may be any that keep to these rules, and one draw needn't show every extreme that they name: `presence`: at least one replica group is present.
All inputs are finite; a program needn't handle non-finite values.
Results may differ from a plain program's by a relative error of at most 0.0075.
Values may be sent and summed in bfloat16 or wider, within the bound.
A program may use at most 64 MiB of HBM per device.

v0:
```python
import jax
import jax.numpy as jnp
from jax import lax
from jax.sharding import PartitionSpec as P


def cut_along(shard, dim, length):
    lengths = shard.shape
    pieces = shard.reshape(*lengths[:dim], length, lengths[dim] // length, *lengths[dim + 1 :])
    return jnp.moveaxis(pieces, dim, 0)


def sum_at_owner(shard, axis, dim):
    length = lax.axis_size(axis)
    pieces = lax.all_to_all(cut_along(shard, dim, length), axis, 0, 0, tiled=True)
    return jnp.sum(pieces.astype(jnp.float32), axis=0)


def in_order(pieces, dim):
    lengths = list(pieces.shape[1:])
    lengths[dim] *= pieces.shape[0]
    return jnp.moveaxis(pieces, 0, dim).reshape(lengths)


def from_everyone(shard, axis):
    copies = jnp.broadcast_to(shard, (lax.axis_size(axis), *shard.shape))
    return lax.all_to_all(copies, axis, split_axis=0, concat_axis=0, tiled=True)


def gathered_copies(shard, axis, dim):
    return in_order(from_everyone(shard, axis), dim)


def shards(deltas, presence, owner_of, outer_params, momentum):
    groups = lax.axis_size("rep")
    rows = deltas.shape[1]
    width = deltas.shape[2] // groups
    present = presence.astype(jnp.float32)
    count = jnp.sum(present)
    local_blocks = deltas[0].reshape(rows, groups, width)
    slotted = jnp.take(local_blocks, owner_of, axis=1).reshape(rows, groups * width)
    own_flag = lax.dynamic_index_in_dim(present, lax.axis_index("rep"), 0, keepdims=False)
    term = slotted.astype(jnp.float32) * own_flag
    total = sum_at_owner(term.astype(jnp.bfloat16), "rep", 1)
    average = total / count
    new_momentum = 0.9 * momentum + average
    new_outer = outer_params - 0.7 * (average + 0.9 * new_momentum)
    shipped = new_outer.astype(jnp.bfloat16)
    gathered = gathered_copies(shipped, "rep", 1)
    inverse = jnp.argsort(owner_of)
    natural = jnp.take(gathered.reshape(rows, groups, width), inverse, axis=1)
    new_weights = natural.reshape(rows, groups * width)
    return (new_weights, new_outer, new_momentum)


def solution(mesh):
    return jax.shard_map(
        shards,
        mesh=mesh,
        in_specs=(P("rep", "shard", None), P(), P(), P("shard", "rep"), P("shard", "rep")),
        out_specs=(P("shard", None), P("shard", "rep"), P("shard", "rep")),
        check_vma=False,
    )
```

profile of v0, /device:TPU:448, one launch (start us, length us, event | category | flops | bytes accessed | tf_op | source)
XLA Modules:
  0.0 86.1 jit_solution(10065740442975020029)
XLA Ops:
  0.6 0.7 compare_select_fusion.1
  1.3 0.7 compare_and_fusion.1
  2.0 0.7 convert_element_type.18
  2.6 1.6 %copy.8 = bf16[1,128,4096]{1,2,0:T(8,128)(2,1)S(1)} copy(bf16[1,128,4096]{2,1,0:T(8,128)(2,1)} %param.7) | data formatting | bytes 2097152 | tf_op args[0]
  4.2 0.7 copy.9
  4.9 0.6 dynamic_slice.4
  5.5 0.7 gather_fusion
  6.3 2.0 %fusion = bf16[32,128,128]{2,1,0:T(8,128)(2,1)} fusion(bf16[32,128,128]{2,1,0:T(8,128)(2,1)S(1)} %gather_fusion, f32[]{:T(128)} %bitcast.2, pred[32]{0:T(512)(128)(4,1)S(1)} %compare_and_fusion.1), kind=kLoop, calls=%fused_computation.4 | loop fusion | flops 2097152 | bytes 2097188 | tf_op jit(solution)/shard_map/transpose | solution.py:10
  8.2 0.0 copy-start.2
  8.2 10.1 %all-to-all-start = ((bf16[32,128,128]{2,1,0:T(8,128)(2,1)}), bf16[32,128,128]{2,1,0:T(8,128)(2,1)S(1)}, u32[]{:S(2)}, u32[]{:S(2)}) async-start(bf16[32,128,128]{2,1,0:T(8,128)(2,1)} %fusion), calls=%async_computation | async-start | bytes 2097152 | tf_op jit(solution)/shard_map/all_to_all | solution.py:15
  18.3 0.0 copy-done.2
  18.3 0.0 copy-start
  18.3 0.0 copy-start.1
  18.4 0.7 convert_reduce_fusion.1
  19.0 27.9 %all-to-all-done = bf16[32,128,128]{2,1,0:T(8,128)(2,1)S(1)} async-done(((bf16[32,128,128]{2,1,0:T(8,128)(2,1)}), bf16[32,128,128]{2,1,0:T(8,128)(2,1)S(1)}, u32[]{:S(2)}, u32[]{:S(2)}) %all-to-all-start) | async-done | bytes 1048608 | tf_op jit(solution)/shard_map/all_to_all | solution.py:15
  46.9 0.2 convert_reduce_fusion
  47.1 0.0 copy-done
  47.1 0.0 copy-done.1
  47.1 1.4 %fusion.1 = (bf16[128,128]{1,0:T(8,128)(2,1)S(1)}, f32[128,128]{1,0:T(8,128)}, f32[128,128]{1,0:T(8,128)}) fusion(f32[128,128]{1,0:T(8,128)S(1)} %copy-done, f32[128,128]{1,0:T(8,128)S(1)} %convert_reduce_fusion, f32[]{:T(128)} %convert_reduce_fusion.1, f32[128,128]{1,0:T(8,128)S(1)} %copy-done.1), kind=kLoop, calls=%fused_computation.16 | loop fusion | flops 131072 | bytes 360452 | tf_op jit(solution)/shard_map/convert_element_type | solution.py:48
  48.5 1.2 %broadcast_in_dim.12 = bf16[32,128,128]{2,1,0:T(8,128)(2,1)} broadcast(bf16[128,128]{1,0:T(8,128)(2,1)S(1)} %get-tuple-element.9), dimensions={1,2} | broadcast | bytes 1081344 | tf_op jit(solution)/shard_map/broadcast_in_dim | solution.py:26
  49.7 0.0 copy-start.3
  49.7 5.2 %all-to-all-start.1 = ((bf16[32,128,128]{2,1,0:T(8,128)(2,1)}), bf16[32,128,128]{2,1,0:T(8,128)(2,1)S(1)}, u32[]{:S(2)}, u32[]{:S(2)}) async-start(bf16[32,128,128]{2,1,0:T(8,128)(2,1)} %broadcast_in_dim.12), calls=%async_computation.1 | async-start | bytes 2097152 | tf_op jit(solution)/shard_map/all_to_all | solution.py:27
  54.9 0.0 copy-done.3
  54.9 1.7 %sort.17 = (s32[32]{0:T(128)}, s32[32]{0:T(128)S(1)}) sort(s32[32]{0:T(128)S(1)} %copy-done.3, s32[32]{0:T(128)S(1)} %iota.4), dimensions={0}, to_apply=%region_2.4 | sort | flops 160 | bytes 512 | tf_op jit(solution)/shard_map/jit(argsort)/sort | solution.py:50
  56.6 26.5 %all-to-all-done.1 = bf16[32,128,128]{2,1,0:T(8,128)(2,1)S(1)} async-done(((bf16[32,128,128]{2,1,0:T(8,128)(2,1)}), bf16[32,128,128]{2,1,0:T(8,128)(2,1)S(1)}, u32[]{:S(2)}, u32[]{:S(2)}) %all-to-all-start.1) | async-done | bytes 1048608 | tf_op jit(solution)/shard_map/all_to_all | solution.py:27
  83.2 0.7 gather_fusion.1
  83.9 0.2 select_bitcast_fusion
  84.1 0.7 copy.10
  84.8 1.3 %copy.11 = bf16[128,4096]{1,0:T(8,128)(2,1)} copy(bf16[128,4096]{0,1:T(8,128)(2,1)S(1)} %bitcast.11) | data formatting | bytes 2097152
  (5 shorter events, 0.0 us)
Async XLA Ops:
  8.2 10.1 %copy-start.2 = (s32[32]{0:T(128)S(1)}, s32[32]{0:T(128)}, u32[]{:S(2)}) copy-start(s32[32]{0:T(128)} %param.8) | copy-start | bytes 388
  8.2 38.7 %all-to-all-start = ((bf16[32,128,128]{2,1,0:T(8,128)(2,1)}), bf16[32,128,128]{2,1,0:T(8,128)(2,1)S(1)}, u32[]{:S(2)}, u32[]{:S(2)}) async-start(bf16[32,128,128]{2,1,0:T(8,128)(2,1)} %fusion), calls=%async_computation | async-start | bytes 2097152 | tf_op jit(solution)/shard_map/all_to_all | solution.py:15
  18.3 28.8 %copy-start = (f32[128,128]{1,0:T(8,128)S(1)}, f32[128,128]{1,0:T(8,128)}, u32[]{:S(2)}) copy-start(f32[128,128]{1,0:T(8,128)} %param.10) | copy-start | bytes 196612
  18.3 28.8 %copy-start.1 = (f32[128,128]{1,0:T(8,128)S(1)}, f32[128,128]{1,0:T(8,128)}, u32[]{:S(2)}) copy-start(f32[128,128]{1,0:T(8,128)} %param.11) | copy-start | bytes 196612
  49.7 5.2 %copy-start.3 = (s32[32]{0:T(128)S(1)}, s32[32]{0:T(128)}, u32[]{:S(2)}) copy-start(s32[32]{0:T(128)} %param.9) | copy-start | bytes 388
  49.7 33.5 %all-to-all-start.1 = ((bf16[32,128,128]{2,1,0:T(8,128)(2,1)}), bf16[32,128,128]{2,1,0:T(8,128)(2,1)S(1)}, u32[]{:S(2)}, u32[]{:S(2)}) async-start(bf16[32,128,128]{2,1,0:T(8,128)(2,1)} %broadcast_in_dim.12), calls=%async_computation.1 | async-start | bytes 2097152 | tf_op jit(solution)/shard_map/all_to_all | solution.py:27
where the time goes:
time: 86.5 us; the launch traced here: 86.1 us
  waiting for transfers between devices  54.4 us (63%)
  starting transfers between devices  15.3 us (18%)
  other arithmetic  8.01 us (9%)
  local copies, waits for them, and re-layouts  7.56 us (9%)
    all_to_all x1, waiting for transfers between devices, sum_at_owner(): lax.all_to_all(cut_along(shard, dim, length), axis, 0, 0, tiled=True)  27.9 us
    all_to_all x1, waiting for transfers between devices, from_everyone(): return lax.all_to_all(copies, axis, split_axis=0, concat_axis=0, tiled=True)  26.5 us
    all_to_all x1, starting transfers between devices, sum_at_owner(): lax.all_to_all(cut_along(shard, dim, length), axis, 0, 0, tiled=True)  10.1 us
    all_to_all x1, starting transfers between devices, from_everyone(): return lax.all_to_all(copies, axis, split_axis=0, concat_axis=0, tiled=True)  5.23 us
    unnamed x10, local copies, waits for them, and re-layouts  2.94 us
    transpose x1, other arithmetic, cut_along(): return jnp.moveaxis(pieces, dim, 0)  1.96 us
  transfers between devices with their start and end apart: 2, of which 2 were waited for; matrix products, arithmetic and copies ran while one was open for 3% of the time, Pallas kernels for 0%

commit v1 on v0

v1 whole, which is shorter than its diff:
```python
import functools

import jax
import jax.numpy as jnp
from jax import lax
from jax.experimental import pallas as pl
from jax.experimental.pallas import tpu as pltpu
from jax.sharding import PartitionSpec as P

MESH = pl.DeviceIdType.MESH
NX, NY = 4, 8
BLOCK = 128
UP = (4, 3, 2, 1)
DOWN = (5, 6, 7, 0)


def kernel(
    deltas, presence, owner_of, outer_in, momentum_in,
    gathered, outer_out, momentum_out,
    delta, buf, near_l, near_r, far, mixed, from_y, to_y,
    outer_v, momentum_v,
    load_sem, far_send, far_recv, l_send, l_recv, r_send, r_recv, y_send, y_recv,
    gy_send, gy_recv, gl_send, gl_recv, gr_send, gr_recv, gf_send, gf_recv,
):
    me = lax.axis_index("rep")
    x = me // NY
    y = me % NY

    def place(dx, dy):
        return ((x + dx) % NX) * NY + (y + dy) % NY

    right, left = place(1, 0), place(NX - 1, 0)

    loads = [
        pltpu.make_async_copy(deltas.at[0, :, b * BLOCK : (b + 1) * BLOCK], delta.at[b], load_sem.at[b])
        for b in range(NX * NY)
    ]
    for load in loads:
        load.start()
    load_outer = pltpu.make_async_copy(outer_in, outer_v, load_sem.at[NX * NY])
    load_momentum = pltpu.make_async_copy(momentum_in, momentum_v, load_sem.at[NX * NY + 1])
    load_outer.start()
    load_momentum.start()

    barrier = pltpu.get_barrier_semaphore()
    partners = [right, left] + [place(0, dy) for dy in range(1, NY)]
    for partner in partners:
        pl.semaphore_signal(barrier, inc=1, device_id={"rep": partner}, device_id_type=MESH)

    present = presence[me].astype(jnp.float32)
    for load in loads:
        load.wait()
    for dx in (2, 1, 3, 0):
        for dy in range(NY):
            block = delta[owner_of[place(dx, dy)]]
            buf[dx, dy] = (block.astype(jnp.float32) * present).astype(jnp.bfloat16)
    pl.semaphore_wait(barrier, len(partners))

    started = []

    def send(src, dst, send_sem, recv_sem, to):
        copy = pltpu.make_async_remote_copy(
            src_ref=src, dst_ref=dst, send_sem=send_sem, recv_sem=recv_sem,
            device_id={"rep": to}, device_id_type=MESH,
        )
        copy.start()
        started.append(copy)
        return copy

    far_copies = {}
    for up, down in zip(UP, DOWN):
        far_copies[up] = send(buf.at[2, up], far.at[up], far_send.at[up], far_recv.at[up], right)
        far_copies[down] = send(buf.at[2, down], far.at[down], far_send.at[down], far_recv.at[down], left)

    count = presence[0]
    for r in range(1, NX * NY):
        count = count + presence[r]

    l_copies, r_copies = {}, {}
    for up, down in zip(UP, DOWN):
        far_copies[up].wait_recv()
        mixed[up] = (far[up].astype(jnp.float32) + buf[1, up].astype(jnp.float32)).astype(jnp.bfloat16)
        l_copies[up] = send(mixed.at[up], near_l.at[up], l_send.at[up], l_recv.at[up], right)
        l_copies[down] = send(buf.at[1, down], near_l.at[down], l_send.at[down], l_recv.at[down], right)
        far_copies[down].wait_recv()
        mixed[down] = (far[down].astype(jnp.float32) + buf[3, down].astype(jnp.float32)).astype(jnp.bfloat16)
        r_copies[down] = send(mixed.at[down], near_r.at[down], r_send.at[down], r_recv.at[down], left)
        r_copies[up] = send(buf.at[3, up], near_r.at[up], r_send.at[up], r_recv.at[up], left)

    y_copies = {}
    own = None
    for pair in zip(UP, DOWN):
        for dy in pair:
            l_copies[dy].wait_recv()
            r_copies[dy].wait_recv()
            total = buf[0, dy].astype(jnp.float32) + (near_l[dy].astype(jnp.float32) + near_r[dy].astype(jnp.float32))
            if dy == 0:
                own = total
            else:
                to_y[dy] = total.astype(jnp.bfloat16)
                y_copies[dy] = send(to_y.at[dy], from_y.at[dy], y_send.at[dy], y_recv.at[dy], place(0, dy))
    total = own
    for dy in (4, 5, 3, 6, 2, 7, 1):
        y_copies[dy].wait_recv()
        total = total + from_y[dy].astype(jnp.float32)

    average = total / count.astype(jnp.float32)
    load_outer.wait()
    load_momentum.wait()
    new_momentum = 0.9 * momentum_v[...] + average
    new_outer = outer_v[...] - 0.7 * (average + 0.9 * new_momentum)
    gathered[me] = new_outer.astype(jnp.bfloat16)

    def row(dx, dy):
        return gathered.at[place(dx, dy)]

    gy_copies, gl_copies, gr_copies, gf_copies = {}, {}, {}, {}
    order = (1, 7, 2, 6, 3, 5, 4)
    for dy in order:
        gy_copies[dy] = send(row(0, 0), row(0, 0), gy_send.at[dy], gy_recv.at[dy], place(0, dy))

    def spread(dy):
        gl_copies[dy] = send(row(0, dy), row(0, dy), gl_send.at[dy], gl_recv.at[dy], right)
        gr_copies[dy] = send(row(0, dy), row(0, dy), gr_send.at[dy], gr_recv.at[dy], left)

    def relay(dy):
        if dy in UP:
            gl_copies[dy].wait_recv()
            gf_copies[dy] = send(row(3, dy), row(3, dy), gf_send.at[dy], gf_recv.at[dy], right)
        else:
            gr_copies[dy].wait_recv()
            gf_copies[dy] = send(row(1, dy), row(1, dy), gf_send.at[dy], gf_recv.at[dy], left)

    spread(0)
    outer_out[...] = new_outer
    momentum_out[...] = new_momentum
    sources = (0,) + order
    for k, dy in enumerate(order):
        gy_copies[NY - dy].wait_recv()
        spread(dy)
        if k >= 2:
            relay(sources[k - 2])
    for dy in sources[len(order) - 2 :]:
        relay(dy)
    for dy in range(NY):
        (gr_copies if dy in UP else gl_copies)[dy].wait_recv()
        gf_copies[dy].wait_recv()

    for copy in started:
        copy.wait_send()


def place_kernel(owner_of, gathered, outer_v, momentum_v, weights_out, outer_out, momentum_out, sems):
    copies = [
        pltpu.make_async_copy(outer_v, outer_out, sems.at[NX * NY]),
        pltpu.make_async_copy(momentum_v, momentum_out, sems.at[NX * NY + 1]),
    ]
    for j in range(NX * NY):
        columns = pl.ds(pl.multiple_of(owner_of[j] * BLOCK, BLOCK), BLOCK)
        copies.append(pltpu.make_async_copy(gathered.at[j], weights_out.at[:, columns], sems.at[j]))
    for copy in copies:
        copy.start()
    for copy in copies:
        copy.wait()


def shards(deltas, presence, owner_of, outer_params, momentum):
    rows, width = deltas.shape[1], deltas.shape[2]
    wide = functools.partial(pltpu.VMEM, dtype=jnp.bfloat16)
    any_space = pl.BlockSpec(memory_space=pl.ANY)
    scalars = pl.BlockSpec(memory_space=pltpu.SMEM)
    vector = pl.BlockSpec(memory_space=pltpu.VMEM)
    sems = pltpu.SemaphoreType.DMA((NY,))
    gathered, new_outer, new_momentum = pl.pallas_call(
        kernel,
        out_shape=(
            pltpu.VMEM((NX * NY, rows, BLOCK), jnp.bfloat16),
            pltpu.VMEM((rows, BLOCK), jnp.float32),
            pltpu.VMEM((rows, BLOCK), jnp.float32),
        ),
        in_specs=[any_space, scalars, scalars, any_space, any_space],
        out_specs=(vector, vector, vector),
        scratch_shapes=[
            wide((NX * NY, rows, BLOCK)),
            wide((NX, NY, rows, BLOCK)),
            wide((NY, rows, BLOCK)),
            wide((NY, rows, BLOCK)),
            wide((NY, rows, BLOCK)),
            wide((NY, rows, BLOCK)),
            wide((NY, rows, BLOCK)),
            wide((NY, rows, BLOCK)),
            pltpu.VMEM((rows, BLOCK), jnp.float32),
            pltpu.VMEM((rows, BLOCK), jnp.float32),
            pltpu.SemaphoreType.DMA((NX * NY + 2,)),
        ]
        + [sems] * 16,
        compiler_params=pltpu.CompilerParams(collective_id=0, has_side_effects=True),
        name="outer_step",
    )(deltas, presence, owner_of, outer_params, momentum)
    in_vmem = functools.partial(pltpu.with_memory_space_constraint, memory_space=pltpu.VMEM)
    return pl.pallas_call(
        place_kernel,
        out_shape=(
            jax.ShapeDtypeStruct((rows, width), jnp.bfloat16),
            jax.ShapeDtypeStruct((rows, BLOCK), jnp.float32),
            jax.ShapeDtypeStruct((rows, BLOCK), jnp.float32),
        ),
        in_specs=[scalars, vector, vector, vector],
        out_specs=(any_space, any_space, any_space),
        scratch_shapes=[pltpu.SemaphoreType.DMA((NX * NY + 2,))],
        name="place_blocks",
    )(owner_of, in_vmem(gathered), in_vmem(new_outer), in_vmem(new_momentum))


def solution(mesh):
    return jax.shard_map(
        shards,
        mesh=mesh,
        in_specs=(P("rep", "shard", None), P(), P(), P("shard", "rep"), P("shard", "rep")),
        out_specs=(P("shard", None), P("shard", "rep"), P("shard", "rep")),
        check_vma=False,
    )
```

time: 86.5 us -> 43.1 us (0.50)
  the two profiles are of different devices: /device:TPU:448 before, /device:TPU:24 now
where the time goes in v1:
time: 43.1 us; the launch traced here: 42.9 us
  Pallas kernels  42.3 us (98%)
  between operations  0.64 us (1%)
    pallas_call x1, Pallas kernels, shards(): pl.pallas_call(kernel, out_shape=(pltpu.VMEM((NX * NY, rows, BLOCK), jnp....  40.3 us
    pallas_call x1, Pallas kernels, shards(): pl.pallas_call(place_kernel, out_shape=(jax.ShapeDtypeStruct((rows, width...  1.95 us

profile of v1, /device:TPU:24, one launch (start us, length us, event | category | flops | bytes accessed | tf_op | source)
XLA Modules:
  0.0 42.9 jit_solution(1455991778299975950)
XLA Ops:
  0.6 40.3 %outer_step.1 = (bf16[32,128,128]{2,1,0:T(8,128)(2,1)S(1)}, f32[128,128]{1,0:T(8,128)S(1)}, f32[128,128]{1,0:T(8,128)S(1)}) custom-call(bf16[1,128,4096]{2,1,0:T(8,128)(2,1)} %deltas.1, s32[32]{0:T(128)} %presence.1, s32[32]{0:T(128)} %owner_of.3, f32[128,128]{1,0:T(8,128)} %outer_in.1, f32[128,128]{1,0:T(8,128)} %momentum_in.1), custom_call_target="tpu_custom_call" | custom-call | tf_op jit(solution)/shard_map/outer_step/pallas_call | solution.py:174
  41.0 2.0 %place_blocks.1 = (bf16[128,4096]{1,0:T(8,128)(2,1)}, f32[128,128]{1,0:T(8,128)}, f32[128,128]{1,0:T(8,128)}) custom-call(s32[32]{0:T(128)} %owner_of.3, bf16[32,128,128]{2,1,0:T(8,128)(2,1)S(1)} %get-tuple-element.6.gathered, f32[128,128]{1,0:T(8,128)S(1)} %get-tuple-element.7.outer_v, f32[128,128]{1,0:T(8,128)S(1)} %get-tuple-element.8.momentum_v), custom_call_target="tpu_custom_call" | custom-call | tf_op jit(solution)/shard_map/place_blocks/pallas_call | solution.py:201

commit v2 on v1

v2 whole, which is shorter than its diff:
```python
import functools

import jax
import jax.numpy as jnp
from jax import lax
from jax.experimental import pallas as pl
from jax.experimental.pallas import tpu as pltpu
from jax.sharding import PartitionSpec as P

SUM_PLAN = ('B', 'F4', 'F3', 'F5', 'F6', 'F2', 'S', 'N4', 'N5', 'N3', 'N6', 'N2', 'T0', 'T4', 'T3', 'T5', 'T2', 'T6', 'M5', 'M3', 'M6', 'M2', 'O', 'Y4', 'Y3', 'Y5', 'Y6', 'Y2')
SPREAD_PLAN = ('f2', 'f6', 'A0', 'f3', 'f5', 'f4', 'f1', 'f7', 'W', 'A6', 'A2', 'G', 'H', 'A5', 'A3', 'A4')
STRAIGHT = (4,)
DIRECT = (4, 3, 5, 2, 6)
MESH = pl.DeviceIdType.MESH
NX, NY = 4, 8
BLOCK = 128
COPIES = 80
UP = (4, 3, 2)
F32, BF16 = jnp.float32, jnp.bfloat16


def kernel(
    deltas, presence, owner_of, outer_in, momentum_in,
    gathered, outer_out, momentum_out,
    delta, buf, side_up, side_down, near_l, near_r, far, mixed, row_out,
    to_y, from_y, outer_v, momentum_v,
    load_sem, send_sems, recv_sems,
):
    me = lax.axis_index("rep")
    x = me // NY
    y = me % NY

    def place(dx, dy):
        return ((x + dx) % NX) * NY + (y + dy) % NY

    right, left = place(1, 0), place(3, 0)
    across, up, down = place(2, 0), place(0, 1), place(0, 7)

    loads = [
        pltpu.make_async_copy(deltas.at[0, :, b * BLOCK : (b + 1) * BLOCK], delta.at[b], load_sem.at[b])
        for b in range(NX * NY)
    ]
    for load in loads:
        load.start()
    load_outer = pltpu.make_async_copy(outer_in, outer_v, load_sem.at[NX * NY])
    load_momentum = pltpu.make_async_copy(momentum_in, momentum_v, load_sem.at[NX * NY + 1])
    load_outer.start()
    load_momentum.start()

    barrier = pltpu.get_barrier_semaphore()
    partners = [right, left, across] + [place(0, dy) for dy in range(1, NY)]
    for partner in partners:
        pl.semaphore_signal(barrier, inc=1, device_id={"rep": partner}, device_id_type=MESH)

    present = presence[me].astype(F32)
    for load in loads:
        load.wait()

    masked = set()

    def term(dy, dx):
        if (dy, dx) not in masked:
            masked.add((dy, dx))
            block = delta[owner_of[place(dx, dy)]]
            buf[dy, dx] = (block.astype(F32) * present).astype(BF16)
        return buf.at[dy, dx]

    started = []

    def send(src, dst, to):
        k = len(started)
        copy = pltpu.make_async_remote_copy(
            src_ref=src, dst_ref=dst, send_sem=send_sems.at[k], recv_sem=recv_sems.at[k],
            device_id={"rep": to}, device_id_type=MESH,
        )
        copy.start()
        started.append(copy)
        return copy

    def drain():
        for copy in started:
            copy.wait_send()

    far_c, l_c, r_c, side_c, own_c, y_c = {}, {}, {}, {}, {}, {}

    def own_row(dx):
        return term(0, dx)[...].astype(F32) + (side_up[dx].astype(F32) + side_down[dx].astype(F32))

    def sum_step(step, dy):
        if step == "B":
            pl.semaphore_wait(barrier, len(partners))
        elif step == "T":
            for dx in range(NX):
                term(dy, dx)
        elif step == "F":
            to = across if dy in STRAIGHT else right if dy in UP else left
            far_c[dy] = send(term(dy, 2), far.at[dy], to)
        elif step == "N":
            if dy in STRAIGHT or dy not in UP:
                l_c[dy] = send(term(dy, 1), near_l.at[dy], right)
            if dy in STRAIGHT or dy in UP:
                r_c[dy] = send(term(dy, 3), near_r.at[dy], left)
        elif step == "M":
            own_term = term(dy, 1 if dy in UP else 3)[...].astype(F32)
            far_c[dy].wait_recv()
            mixed[dy] = (far[dy].astype(F32) + own_term).astype(BF16)
            if dy in UP:
                l_c[dy] = send(mixed.at[dy], near_l.at[dy], right)
            else:
                r_c[dy] = send(mixed.at[dy], near_r.at[dy], left)
        elif step == "S":
            for side, src, dst, to in ((0, 1, side_up, up), (1, 7, side_down, down)):
                for dx in range(NX):
                    term(src, dx)
                side_c[side] = send(buf.at[src], dst, to)
        elif step == "O":
            side_c[0].wait_recv()
            side_c[1].wait_recv()
            for dx, dst, to in ((2, far.at[0], across), (1, near_l.at[0], right), (3, near_r.at[0], left)):
                row_out[dx] = own_row(dx).astype(BF16)
                own_c[dx] = send(row_out.at[dx], dst, to)
        elif step == "Y":
            own_term = term(dy, 0)[...].astype(F32)
            l_c[dy].wait_recv()
            r_c[dy].wait_recv()
            x_total = own_term + (near_l[dy].astype(F32) + near_r[dy].astype(F32))
            if dy in STRAIGHT:
                far_c[dy].wait_recv()
                x_total = x_total + far[dy].astype(F32)
            to_y[dy] = x_total.astype(BF16)
            y_c[dy] = send(to_y.at[dy], from_y.at[dy], place(0, dy))

    for step in SUM_PLAN:
        sum_step(step[0], int(step[1:] or 0))

    count = presence[0]
    for r in range(1, NX * NY):
        count = count + presence[r]
    total = own_row(0)
    load_outer.wait()
    load_momentum.wait()
    for copy in own_c.values():
        copy.wait_recv()
    total = total + (near_l[0].astype(F32) + near_r[0].astype(F32) + far[0].astype(F32))
    for dy, copy in y_c.items():
        copy.wait_recv()
        total = total + from_y[dy].astype(F32)

    average = total / count.astype(F32)
    new_momentum = 0.9 * momentum_v[...] + average
    new_outer = outer_v[...] - 0.7 * (average + 0.9 * new_momentum)
    gathered[me] = new_outer.astype(BF16)

    def row(dx, dy):
        return gathered.at[place(dx, dy)]

    def forward(dx, dy, to):
        return send(row(dx, dy), row(dx, dy), to)

    from_l, from_r, relay_c, across_c, fan_c, sides = {}, {}, {}, {}, {}, []

    def spread_step(step, dy):
        if step == "f":
            fan_c[dy] = forward(0, 0, place(0, dy))
        elif step == "A":
            if dy:
                fan_c[NY - dy].wait_recv()
            from_l[dy] = forward(0, dy, right)
            from_r[dy] = forward(0, dy, left)
            if dy in DIRECT or dy == 0:
                across_c[dy] = forward(0, dy, across)
        elif step == "G":
            from_l[0].wait_recv()
            sides.extend([forward(3, 0, up), forward(3, 0, down)])
            from_r[0].wait_recv()
            sides.extend([forward(1, 0, up), forward(1, 0, down)])
        elif step == "H":
            across_c[0].wait_recv()
            sides.extend([forward(2, 0, up), forward(2, 0, down)])
        elif step == "R":
            if dy in UP:
                from_l[dy].wait_recv()
                relay_c[dy] = forward(3, dy, right)
            else:
                from_r[dy].wait_recv()
                relay_c[dy] = forward(1, dy, left)
        elif step == "W":
            outer_out[...] = new_outer
            momentum_out[...] = new_momentum

    for step in SPREAD_PLAN:
        spread_step(step[0], int(step[1:] or 0))
    fan_c[1].wait_recv()
    fan_c[7].wait_recv()
    for dy in (6, 2, 5, 3, 4):
        if dy in DIRECT:
            from_l[dy].wait_recv()
            from_r[dy].wait_recv()
            across_c[dy].wait_recv()
        else:
            (from_r if dy in UP else from_l)[dy].wait_recv()
            relay_c[dy].wait_recv()
    for copy in sides:
        copy.wait_recv()
    drain()
    assert len(started) <= COPIES


def place_kernel(owner_of, gathered, outer_v, momentum_v, weights_out, outer_out, momentum_out, sems):
    copies = [
        pltpu.make_async_copy(outer_v, outer_out, sems.at[NX * NY]),
        pltpu.make_async_copy(momentum_v, momentum_out, sems.at[NX * NY + 1]),
    ]
    for j in range(NX * NY):
        columns = pl.ds(pl.multiple_of(owner_of[j] * BLOCK, BLOCK), BLOCK)
        copies.append(pltpu.make_async_copy(gathered.at[j], weights_out.at[:, columns], sems.at[j]))
    for copy in copies:
        copy.start()
    for copy in copies:
        copy.wait()


def shards(deltas, presence, owner_of, outer_params, momentum):
    rows, width = deltas.shape[1], deltas.shape[2]
    any_space = pl.BlockSpec(memory_space=pl.ANY)
    scalars = pl.BlockSpec(memory_space=pltpu.SMEM)
    vector = pl.BlockSpec(memory_space=pltpu.VMEM)

    def blocks(*shape, dtype=BF16):
        return pltpu.VMEM((*shape, rows, BLOCK), dtype)

    gathered, new_outer, new_momentum = pl.pallas_call(
        kernel,
        out_shape=(blocks(NX * NY), blocks(dtype=F32), blocks(dtype=F32)),
        in_specs=[any_space, scalars, scalars, any_space, any_space],
        out_specs=(vector, vector, vector),
        scratch_shapes=[
            blocks(NX * NY),
            blocks(NY, NX),
            blocks(NX),
            blocks(NX),
            blocks(NY),
            blocks(NY),
            blocks(NY),
            blocks(NY),
            blocks(NX),
            blocks(NY),
            blocks(NY),
            blocks(dtype=F32),
            blocks(dtype=F32),
            pltpu.SemaphoreType.DMA((NX * NY + 2,)),
            pltpu.SemaphoreType.DMA((COPIES,)),
            pltpu.SemaphoreType.DMA((COPIES,)),
        ],
        compiler_params=pltpu.CompilerParams(collective_id=0, has_side_effects=True),
        name="outer_step",
    )(deltas, presence, owner_of, outer_params, momentum)
    in_vmem = functools.partial(pltpu.with_memory_space_constraint, memory_space=pltpu.VMEM)
    return pl.pallas_call(
        place_kernel,
        out_shape=(
            jax.ShapeDtypeStruct((rows, width), BF16),
            jax.ShapeDtypeStruct((rows, BLOCK), F32),
            jax.ShapeDtypeStruct((rows, BLOCK), F32),
        ),
        in_specs=[scalars, vector, vector, vector],
        out_specs=(any_space, any_space, any_space),
        scratch_shapes=[pltpu.SemaphoreType.DMA((NX * NY + 2,))],
        name="place_blocks",
    )(owner_of, in_vmem(gathered), in_vmem(new_outer), in_vmem(new_momentum))


def solution(mesh):
    return jax.shard_map(
        shards,
        mesh=mesh,
        in_specs=(P("rep", "shard", None), P(), P(), P("shard", "rep"), P("shard", "rep")),
        out_specs=(P("shard", None), P("shard", "rep"), P("shard", "rep")),
        check_vma=False,
    )
```

time: 43.1 us -> 38.6 us (0.90)
  the two profiles are of different devices: /device:TPU:24 before, /device:TPU:448 now
where the time goes in v2:
time: 38.6 us; the launch traced here: 38.4 us
  Pallas kernels  37.8 us (98%)
  between operations  0.64 us (2%)
    pallas_call x1, Pallas kernels, shards(): pl.pallas_call(kernel, out_shape=(blocks(NX * NY), blocks(dtype=F32), blo...  35.8 us
    pallas_call x1, Pallas kernels, shards(): pl.pallas_call(place_kernel, out_shape=(jax.ShapeDtypeStruct((rows, width...  1.95 us

profile of v2, /device:TPU:448, one launch (start us, length us, event | category | flops | bytes accessed | tf_op | source)
XLA Modules:
  0.0 38.4 jit_solution(5862735836526422828)
XLA Ops:
  0.6 35.8 %outer_step.1 = (bf16[32,128,128]{2,1,0:T(8,128)(2,1)S(1)}, f32[128,128]{1,0:T(8,128)S(1)}, f32[128,128]{1,0:T(8,128)S(1)}) custom-call(bf16[1,128,4096]{2,1,0:T(8,128)(2,1)} %deltas.1, s32[32]{0:T(128)} %presence.1, s32[32]{0:T(128)} %owner_of.3, f32[128,128]{1,0:T(8,128)} %outer_in.1, f32[128,128]{1,0:T(8,128)} %momentum_in.1), custom_call_target="tpu_custom_call" | custom-call | tf_op jit(solution)/shard_map/outer_step/pallas_call | solution.py:232
  36.5 2.0 %place_blocks.1 = (bf16[128,4096]{1,0:T(8,128)(2,1)}, f32[128,128]{1,0:T(8,128)}, f32[128,128]{1,0:T(8,128)}) custom-call(s32[32]{0:T(128)} %owner_of.3, bf16[32,128,128]{2,1,0:T(8,128)(2,1)S(1)} %get-tuple-element.6.gathered, f32[128,128]{1,0:T(8,128)S(1)} %get-tuple-element.7.outer_v, f32[128,128]{1,0:T(8,128)S(1)} %get-tuple-element.8.momentum_v), custom_call_target="tpu_custom_call" | custom-call | tf_op jit(solution)/shard_map/place_blocks/pallas_call | solution.py:259

commit v3 on v2

v3 whole, which is shorter than its diff:
```python
import functools

import jax
import jax.numpy as jnp
from jax import lax
from jax.experimental import pallas as pl
from jax.experimental.pallas import tpu as pltpu
from jax.sharding import PartitionSpec as P

PLAN = ('F40', 'F30', 'F50', 'F60', 'F20', 'S00', 'N40', 'N50', 'N30', 'N60', 'N20', 'F41', 'F31', 'F51', 'F61', 'F21', 'S01', 'N41', 'N51', 'N31', 'N61', 'N21', 'T00', 'T40', 'T30', 'T50', 'T20', 'T60', 'T01', 'T41', 'T31', 'T51', 'T21', 'T61', 'M50', 'M30', 'M60', 'M20', 'O00', 'Y40', 'M51', 'M31', 'M61', 'M21', 'Y30', 'Y50', 'Y60', 'Y20', 'O01', 'Y41', 'Y31', 'Y51', 'L00', 'Y61', 'Y21', 'D00', 'D01', 'A60', 'A20', 'G00', 'A50', 'A30', 'A40', 'A61', 'A21', 'G01', 'A51', 'A31', 'A41', 'E00', 'E01')
PARTS = 2
MESH = pl.DeviceIdType.MESH
NX, NY = 4, 8
BLOCK = 128
COPIES = 60 * PARTS
UP = (4, 3, 2)
F32, BF16 = jnp.float32, jnp.bfloat16


def kernel(
    deltas, presence, owner_of, outer_in, momentum_in,
    gathered, outer_out, momentum_out,
    delta, buf, side_up, side_down, near_l, near_r, far, mixed, row_out,
    to_y, from_y, outer_v, momentum_v,
    load_sem, send_sems, recv_sems,
):
    me = lax.axis_index("rep")
    x = me // NY
    y = me % NY

    def place(dx, dy):
        return ((x + dx) % NX) * NY + (y + dy) % NY

    right, left = place(1, 0), place(3, 0)
    across, up, down = place(2, 0), place(0, 1), place(0, 7)

    loads = [
        pltpu.make_async_copy(deltas.at[0, :, b * BLOCK : (b + 1) * BLOCK], delta.at[b], load_sem.at[b])
        for b in range(NX * NY)
    ]
    for load in loads:
        load.start()
    load_outer = pltpu.make_async_copy(outer_in, outer_v, load_sem.at[NX * NY])
    load_momentum = pltpu.make_async_copy(momentum_in, momentum_v, load_sem.at[NX * NY + 1])
    load_outer.start()
    load_momentum.start()

    barrier = pltpu.get_barrier_semaphore()
    partners = [right, left, across] + [place(0, dy) for dy in range(1, NY)]
    for partner in partners:
        pl.semaphore_signal(barrier, inc=1, device_id={"rep": partner}, device_id_type=MESH)

    present = presence[me].astype(F32)
    for load in loads:
        load.wait()

    masked = set()
    height = BLOCK // PARTS

    def rows_of(h):
        return pl.ds(h * height, height)

    def term(dy, dx, h):
        rows = rows_of(h)
        if (dy, dx, h) not in masked:
            masked.add((dy, dx, h))
            block = delta[owner_of[place(dx, dy)]][h * height : (h + 1) * height]
            buf[dy, dx, rows] = (block.astype(F32) * present).astype(BF16)
        return buf.at[dy, dx, rows]

    started = []

    def send(src, dst, to):
        k = len(started)
        copy = pltpu.make_async_remote_copy(
            src_ref=src, dst_ref=dst, send_sem=send_sems.at[k], recv_sem=recv_sems.at[k],
            device_id={"rep": to}, device_id_type=MESH,
        )
        copy.start()
        started.append(copy)
        return copy

    def drain():
        for copy in started:
            copy.wait_send()

    c = {}
    count = presence[0]
    for r in range(1, NX * NY):
        count = count + presence[r]

    def wide(ref):
        return ref[...].astype(F32)

    def own_row(dx, h):
        rows = rows_of(h)
        return wide(term(0, dx, h)) + (wide(side_up.at[dx, rows]) + wide(side_down.at[dx, rows]))

    def block_ref(dx, dy, h):
        return gathered.at[place(dx, dy), rows_of(h)]

    def forward(dx, dy, h, to):
        ref = block_ref(dx, dy, h)
        return send(ref, ref, to)

    def spread(dy, h):
        c["right", dy, h] = forward(0, dy, h, right)
        c["left", dy, h] = forward(0, dy, h, left)
        c["across", dy, h] = forward(0, dy, h, across)

    def finish_sum(h):
        rows = rows_of(h)
        total = own_row(0, h)
        for dx in (1, 2, 3):
            c["own", dx, h].wait_recv()
        total = total + (wide(near_l.at[0, rows]) + wide(near_r.at[0, rows]) + wide(far.at[0, rows]))
        for dy in (4, 3, 5, 6, 2):
            c["y", dy, h].wait_recv()
            total = total + wide(from_y.at[dy, rows])
        average = total / count.astype(F32)
        new_momentum = 0.9 * momentum_v[rows] + average
        new_outer = outer_v[rows] - 0.7 * (average + 0.9 * new_momentum)
        gathered[me, rows] = new_outer.astype(BF16)
        for dy in (2, 6, 0, 3, 5, 4, 1, 7):
            if dy:
                c["fan", dy, h] = forward(0, 0, h, place(0, dy))
            else:
                spread(0, h)
        outer_out[rows] = new_outer
        momentum_out[rows] = new_momentum

    def do_step(step, dy, h):
        rows = rows_of(h)
        if step == "F":
            to = across if dy == 4 else right if dy in UP else left
            c["far", dy, h] = send(term(dy, 2, h), far.at[dy, rows], to)
        elif step == "N":
            if dy == 4 or dy not in UP:
                c["l", dy, h] = send(term(dy, 1, h), near_l.at[dy, rows], right)
            if dy in UP:
                c["r", dy, h] = send(term(dy, 3, h), near_r.at[dy, rows], left)
        elif step == "M":
            own_term = wide(term(dy, 1 if dy in UP else 3, h))
            c["far", dy, h].wait_recv()
            mixed[dy, rows] = (wide(far.at[dy, rows]) + own_term).astype(BF16)
            if dy in UP:
                c["l", dy, h] = send(mixed.at[dy, rows], near_l.at[dy, rows], right)
            else:
                c["r", dy, h] = send(mixed.at[dy, rows], near_r.at[dy, rows], left)
        elif step == "S":
            for src, dst, to in ((1, side_up, up), (7, side_down, down)):
                for dx in range(NX):
                    term(src, dx, h)
                c["side", src, h] = send(buf.at[src, :, rows], dst.at[:, rows], to)
        elif step == "O":
            c["side", 1, h].wait_recv()
            c["side", 7, h].wait_recv()
            for dx, dst, to in ((2, far, across), (1, near_l, right), (3, near_r, left)):
                row_out[dx, rows] = own_row(dx, h).astype(BF16)
                c["own", dx, h] = send(row_out.at[dx, rows], dst.at[0, rows], to)
        elif step == "T":
            term(dy, 0, h)
            if dy == 0:
                for dx in range(NX):
                    term(0, dx, h)
            elif dy != 4:
                term(dy, 1 if dy in UP else 3, h)
        elif step == "Y":
            own_term = wide(term(dy, 0, h))
            c["l", dy, h].wait_recv()
            c["r", dy, h].wait_recv()
            x_total = own_term + (wide(near_l.at[dy, rows]) + wide(near_r.at[dy, rows]))
            if dy == 4:
                c["far", dy, h].wait_recv()
                x_total = x_total + wide(far.at[dy, rows])
            to_y[dy, rows] = x_total.astype(BF16)
            c["y", dy, h] = send(to_y.at[dy, rows], from_y.at[dy, rows], place(0, dy))
        elif step == "L":
            load_outer.wait()
            load_momentum.wait()
        elif step == "D":
            finish_sum(h)
        elif step == "A":
            c["fan", NY - dy, h].wait_recv()
            spread(dy, h)
        elif step == "G":
            for name, dx in (("left", 1), ("right", 3), ("across", 2)):
                c[name, 0, h].wait_recv()
                c["side_up", dx, h] = forward(dx, 0, h, up)
                c["side_down", dx, h] = forward(dx, 0, h, down)
        elif step == "E":
            c["fan", 1, h].wait_recv()
            c["fan", 7, h].wait_recv()
            for dy in (6, 2, 5, 3, 4):
                for name in ("right", "left", "across"):
                    c[name, dy, h].wait_recv()
            for dx in (1, 2, 3):
                c["side_up", dx, h].wait_recv()
                c["side_down", dx, h].wait_recv()

    pl.semaphore_wait(barrier, len(partners))
    for token in PLAN:
        do_step(token[0], int(token[1]), int(token[2]))
    drain()
    assert len(started) <= COPIES


def place_kernel(owner_of, gathered, outer_v, momentum_v, weights_out, outer_out, momentum_out, sems):
    copies = [
        pltpu.make_async_copy(outer_v, outer_out, sems.at[NX * NY]),
        pltpu.make_async_copy(momentum_v, momentum_out, sems.at[NX * NY + 1]),
    ]
    for j in range(NX * NY):
        columns = pl.ds(pl.multiple_of(owner_of[j] * BLOCK, BLOCK), BLOCK)
        copies.append(pltpu.make_async_copy(gathered.at[j], weights_out.at[:, columns], sems.at[j]))
    for copy in copies:
        copy.start()
    for copy in copies:
        copy.wait()


def shards(deltas, presence, owner_of, outer_params, momentum):
    rows, width = deltas.shape[1], deltas.shape[2]
    any_space = pl.BlockSpec(memory_space=pl.ANY)
    scalars = pl.BlockSpec(memory_space=pltpu.SMEM)
    vector = pl.BlockSpec(memory_space=pltpu.VMEM)

    def blocks(*shape, dtype=BF16):
        return pltpu.VMEM((*shape, rows, BLOCK), dtype)

    gathered, new_outer, new_momentum = pl.pallas_call(
        kernel,
        out_shape=(blocks(NX * NY), blocks(dtype=F32), blocks(dtype=F32)),
        in_specs=[any_space, scalars, scalars, any_space, any_space],
        out_specs=(vector, vector, vector),
        scratch_shapes=[
            blocks(NX * NY),
            blocks(NY, NX),
            blocks(NX),
            blocks(NX),
            blocks(NY),
            blocks(NY),
            blocks(NY),
            blocks(NY),
            blocks(NX),
            blocks(NY),
            blocks(NY),
            blocks(dtype=F32),
            blocks(dtype=F32),
            pltpu.SemaphoreType.DMA((NX * NY + 2,)),
            pltpu.SemaphoreType.DMA((COPIES,)),
            pltpu.SemaphoreType.DMA((COPIES,)),
        ],
        compiler_params=pltpu.CompilerParams(collective_id=0, has_side_effects=True),
        name="outer_step",
    )(deltas, presence, owner_of, outer_params, momentum)
    in_vmem = functools.partial(pltpu.with_memory_space_constraint, memory_space=pltpu.VMEM)
    return pl.pallas_call(
        place_kernel,
        out_shape=(
            jax.ShapeDtypeStruct((rows, width), BF16),
            jax.ShapeDtypeStruct((rows, BLOCK), F32),
            jax.ShapeDtypeStruct((rows, BLOCK), F32),
        ),
        in_specs=[scalars, vector, vector, vector],
        out_specs=(any_space, any_space, any_space),
        scratch_shapes=[pltpu.SemaphoreType.DMA((NX * NY + 2,))],
        name="place_blocks",
    )(owner_of, in_vmem(gathered), in_vmem(new_outer), in_vmem(new_momentum))


def solution(mesh):
    return jax.shard_map(
        shards,
        mesh=mesh,
        in_specs=(P("rep", "shard", None), P(), P(), P("shard", "rep"), P("shard", "rep")),
        out_specs=(P("shard", None), P("shard", "rep"), P("shard", "rep")),
        check_vma=False,
    )
```

time: 38.6 us -> 37.7 us (0.977)
  Pallas kernels: 37.8 us -> 36.5 us
    pallas_call x1, Pallas kernels: 35.8 us -> 34.6 us  [shards(): pl.pallas_call(kernel, out_shape=(blocks(NX * NY), blocks(dtype=F32), blo...]
where the time goes in v3:
time: 37.7 us; the launch traced here: 37.2 us
  Pallas kernels  36.5 us (97%)
  between operations  0.64 us (2%)
    pallas_call x1, Pallas kernels, shards(): pl.pallas_call(kernel, out_shape=(blocks(NX * NY), blocks(dtype=F32), blo...  34.6 us
    pallas_call x1, Pallas kernels, shards(): pl.pallas_call(place_kernel, out_shape=(jax.ShapeDtypeStruct((rows, width...  1.95 us

profile of v3, /device:TPU:448, one launch (start us, length us, event | category | flops | bytes accessed | tf_op | source)
XLA Modules:
  0.0 37.2 jit_solution(15681471671119718632)
XLA Ops:
  0.6 34.6 %outer_step.1 = (bf16[32,128,128]{2,1,0:T(8,128)(2,1)S(1)}, f32[128,128]{1,0:T(8,128)S(1)}, f32[128,128]{1,0:T(8,128)S(1)}) custom-call(bf16[1,128,4096]{2,1,0:T(8,128)(2,1)} %deltas.1, s32[32]{0:T(128)} %presence.1, s32[32]{0:T(128)} %owner_of.3, f32[128,128]{1,0:T(8,128)} %outer_in.1, f32[128,128]{1,0:T(8,128)} %momentum_in.1), custom_call_target="tpu_custom_call" | custom-call | tf_op jit(solution)/shard_map/outer_step/pallas_call | solution.py:231
  35.2 2.0 %place_blocks.1 = (bf16[128,4096]{1,0:T(8,128)(2,1)}, f32[128,128]{1,0:T(8,128)}, f32[128,128]{1,0:T(8,128)}) custom-call(s32[32]{0:T(128)} %owner_of.3, bf16[32,128,128]{2,1,0:T(8,128)(2,1)S(1)} %get-tuple-element.6.gathered, f32[128,128]{1,0:T(8,128)S(1)} %get-tuple-element.7.outer_v, f32[128,128]{1,0:T(8,128)S(1)} %get-tuple-element.8.momentum_v), custom_call_target="tpu_custom_call" | custom-call | tf_op jit(solution)/shard_map/place_blocks/pallas_call | solution.py:258

commit v4 on v3

--- a/solution.py
+++ b/solution.py
@@ -12,6 +12,7 @@
 MESH = pl.DeviceIdType.MESH
 NX, NY = 4, 8
 BLOCK = 128
+SLABS = 4
 COPIES = 60 * PARTS
 UP = (4, 3, 2)
 F32, BF16 = jnp.float32, jnp.bfloat16
@@ -205,16 +206,21 @@
     assert len(started) <= COPIES
 
 
-def place_kernel(owner_of, gathered, outer_v, momentum_v, weights_out, outer_out, momentum_out, sems):
+def place_kernel(owner_of, gathered, outer_v, momentum_v, weights_out, outer_out, momentum_out, natural, sems):
     copies = [
-        pltpu.make_async_copy(outer_v, outer_out, sems.at[NX * NY]),
-        pltpu.make_async_copy(momentum_v, momentum_out, sems.at[NX * NY + 1]),
+        pltpu.make_async_copy(outer_v, outer_out, sems.at[SLABS]),
+        pltpu.make_async_copy(momentum_v, momentum_out, sems.at[SLABS + 1]),
     ]
-    for j in range(NX * NY):
-        columns = pl.ds(pl.multiple_of(owner_of[j] * BLOCK, BLOCK), BLOCK)
-        copies.append(pltpu.make_async_copy(gathered.at[j], weights_out.at[:, columns], sems.at[j]))
     for copy in copies:
         copy.start()
+    for slab in range(SLABS):
+        rows = pl.ds(slab * (BLOCK // SLABS), BLOCK // SLABS)
+        for j in range(NX * NY):
+            columns = pl.ds(pl.multiple_of(owner_of[j] * BLOCK, BLOCK), BLOCK)
+            natural[rows, columns] = gathered[j, rows]
+        copy = pltpu.make_async_copy(natural.at[rows], weights_out.at[rows], sems.at[slab])
+        copy.start()
+        copies.append(copy)
     for copy in copies:
         copy.wait()
 
@@ -264,7 +270,7 @@
         ),
         in_specs=[scalars, vector, vector, vector],
         out_specs=(any_space, any_space, any_space),
-        scratch_shapes=[pltpu.SemaphoreType.DMA((NX * NY + 2,))],
+        scratch_shapes=[pltpu.VMEM((rows, width), BF16), pltpu.SemaphoreType.DMA((SLABS + 2,))],
         name="place_blocks",
     )(owner_of, in_vmem(gathered), in_vmem(new_outer), in_vmem(new_momentum))
 

time: 37.7 us -> 37.6 us (level)
  no operation moved by 1% of the time
where the time goes in v4:
time: 37.6 us; the launch traced here: 37 us
  Pallas kernels  36.3 us (97%)
  between operations  0.64 us (2%)
    pallas_call x1, Pallas kernels, shards(): pl.pallas_call(kernel, out_shape=(blocks(NX * NY), blocks(dtype=F32), blo...  34.6 us
    pallas_call x1, Pallas kernels, shards(): pl.pallas_call(place_kernel, out_shape=(jax.ShapeDtypeStruct((rows, width...  1.77 us

profile of v4, /device:TPU:448, one launch (start us, length us, event | category | flops | bytes accessed | tf_op | source)
XLA Modules:
  0.0 37.0 jit_solution(12767946981883814806)
XLA Ops:
  0.6 34.6 %outer_step.1 = (bf16[32,128,128]{2,1,0:T(8,128)(2,1)S(1)}, f32[128,128]{1,0:T(8,128)S(1)}, f32[128,128]{1,0:T(8,128)S(1)}) custom-call(bf16[1,128,4096]{2,1,0:T(8,128)(2,1)} %deltas.1, s32[32]{0:T(128)} %presence.1, s32[32]{0:T(128)} %owner_of.3, f32[128,128]{1,0:T(8,128)} %outer_in.1, f32[128,128]{1,0:T(8,128)} %momentum_in.1), custom_call_target="tpu_custom_call" | custom-call | tf_op jit(solution)/shard_map/outer_step/pallas_call | solution.py:237
  35.2 1.8 %place_blocks.1 = (bf16[128,4096]{1,0:T(8,128)(2,1)}, f32[128,128]{1,0:T(8,128)}, f32[128,128]{1,0:T(8,128)}) custom-call(s32[32]{0:T(128)} %owner_of.3, bf16[32,128,128]{2,1,0:T(8,128)(2,1)S(1)} %get-tuple-element.6.gathered, f32[128,128]{1,0:T(8,128)S(1)} %get-tuple-element.7.outer_v, f32[128,128]{1,0:T(8,128)S(1)} %get-tuple-element.8.momentum_v), custom_call_target="tpu_custom_call" | custom-call | tf_op jit(solution)/shard_map/place_blocks/pallas_call | solution.py:264

commit v5 on v4

--- a/solution.py
+++ b/solution.py
@@ -7,7 +7,7 @@
 from jax.experimental.pallas import tpu as pltpu
 from jax.sharding import PartitionSpec as P
 
-PLAN = ('F40', 'F30', 'F50', 'F60', 'F20', 'S00', 'N40', 'N50', 'N30', 'N60', 'N20', 'F41', 'F31', 'F51', 'F61', 'F21', 'S01', 'N41', 'N51', 'N31', 'N61', 'N21', 'T00', 'T40', 'T30', 'T50', 'T20', 'T60', 'T01', 'T41', 'T31', 'T51', 'T21', 'T61', 'M50', 'M30', 'M60', 'M20', 'O00', 'Y40', 'M51', 'M31', 'M61', 'M21', 'Y30', 'Y50', 'Y60', 'Y20', 'O01', 'Y41', 'Y31', 'Y51', 'L00', 'Y61', 'Y21', 'D00', 'D01', 'A60', 'A20', 'G00', 'A50', 'A30', 'A40', 'A61', 'A21', 'G01', 'A51', 'A31', 'A41', 'E00', 'E01')
+PLAN = ('F40', 'F30', 'S00', 'F50', 'F60', 'F20', 'N40', 'N50', 'N30', 'N60', 'N20', 'F41', 'F31', 'S01', 'F51', 'F61', 'F21', 'N41', 'N51', 'N31', 'N61', 'N21', 'T00', 'T40', 'T30', 'T50', 'T20', 'T60', 'T01', 'T41', 'T31', 'T51', 'T21', 'T61', 'M50', 'M30', 'M60', 'M20', 'O00', 'H00', 'Y40', 'M51', 'M31', 'M61', 'M21', 'Y30', 'Y50', 'Y60', 'Y20', 'O01', 'Y41', 'Y31', 'Y51', 'L00', 'Y61', 'Y21', 'D00', 'D01', 'A60', 'A20', 'G00', 'A50', 'A30', 'A40', 'A61', 'A21', 'G01', 'A51', 'A31', 'A41', 'E00', 'E01')
 PARTS = 2
 MESH = pl.DeviceIdType.MESH
 NX, NY = 4, 8
@@ -23,7 +23,7 @@
     gathered, outer_out, momentum_out,
     delta, buf, side_up, side_down, near_l, near_r, far, mixed, row_out,
     to_y, from_y, outer_v, momentum_v,
-    load_sem, send_sems, recv_sems,
+    load_sem, send_sems, recv_sems, ready_sem,
 ):
     me = lax.axis_index("rep")
     x = me // NY
@@ -47,7 +47,8 @@
     load_momentum.start()
 
     barrier = pltpu.get_barrier_semaphore()
-    partners = [right, left, across] + [place(0, dy) for dy in range(1, NY)]
+    near = (1, 2, 6, 7)
+    partners = [right, left, across] + [place(0, dy) for dy in near]
     for partner in partners:
         pl.semaphore_signal(barrier, inc=1, device_id={"rep": partner}, device_id_type=MESH)
 
@@ -176,6 +177,8 @@
                 x_total = x_total + wide(far.at[dy, rows])
             to_y[dy, rows] = x_total.astype(BF16)
             c["y", dy, h] = send(to_y.at[dy, rows], from_y.at[dy, rows], place(0, dy))
+        elif step == "H":
+            pl.semaphore_wait(ready_sem, 2)
         elif step == "L":
             load_outer.wait()
             load_momentum.wait()
@@ -200,6 +203,8 @@
                 c["side_down", dx, h].wait_recv()
 
     pl.semaphore_wait(barrier, len(partners))
+    for dy in (2, 6):
+        pl.semaphore_signal(ready_sem, inc=1, device_id={"rep": place(0, dy)}, device_id_type=MESH)
     for token in PLAN:
         do_step(token[0], int(token[1]), int(token[2]))
     drain()
@@ -256,6 +261,7 @@
             pltpu.SemaphoreType.DMA((NX * NY + 2,)),
             pltpu.SemaphoreType.DMA((COPIES,)),
             pltpu.SemaphoreType.DMA((COPIES,)),
+            pltpu.SemaphoreType.REGULAR,
         ],
         compiler_params=pltpu.CompilerParams(collective_id=0, has_side_effects=True),
         name="outer_step",

time: 37.6 us -> 36.5 us (0.971); the launches traced: 37 us -> 36.3 us
  Pallas kernels: 36.3 us -> 35.6 us
    pallas_call x1, Pallas kernels: 34.6 us -> 33.9 us  [shards(): pl.pallas_call(kernel, out_shape=(blocks(NX * NY), blocks(dtype=F32), blo...]
where the time goes in v5:
time: 36.5 us; the launch traced here: 36.3 us
  Pallas kernels  35.6 us (98%)
  between operations  0.64 us (2%)
    pallas_call x1, Pallas kernels, shards(): pl.pallas_call(kernel, out_shape=(blocks(NX * NY), blocks(dtype=F32), blo...  33.9 us
    pallas_call x1, Pallas kernels, shards(): pl.pallas_call(place_kernel, out_shape=(jax.ShapeDtypeStruct((rows, width...  1.78 us

profile of v5, /device:TPU:448, one launch (start us, length us, event | category | flops | bytes accessed | tf_op | source)
XLA Modules:
  0.0 36.3 jit_solution(13293196503669147608)
XLA Ops:
  0.6 33.9 %outer_step.1 = (bf16[32,128,128]{2,1,0:T(8,128)(2,1)S(1)}, f32[128,128]{1,0:T(8,128)S(1)}, f32[128,128]{1,0:T(8,128)S(1)}) custom-call(bf16[1,128,4096]{2,1,0:T(8,128)(2,1)} %deltas.1, s32[32]{0:T(128)} %presence.1, s32[32]{0:T(128)} %owner_of.3, f32[128,128]{1,0:T(8,128)} %outer_in.1, f32[128,128]{1,0:T(8,128)} %momentum_in.1), custom_call_target="tpu_custom_call" | custom-call | tf_op jit(solution)/shard_map/outer_step/pallas_call | solution.py:242
  34.5 1.8 %place_blocks.1 = (bf16[128,4096]{1,0:T(8,128)(2,1)}, f32[128,128]{1,0:T(8,128)}, f32[128,128]{1,0:T(8,128)}) custom-call(s32[32]{0:T(128)} %owner_of.3, bf16[32,128,128]{2,1,0:T(8,128)(2,1)S(1)} %get-tuple-element.6.gathered, f32[128,128]{1,0:T(8,128)S(1)} %get-tuple-element.7.outer_v, f32[128,128]{1,0:T(8,128)S(1)} %get-tuple-element.8.momentum_v), custom_call_target="tpu_custom_call" | custom-call | tf_op jit(solution)/shard_map/place_blocks/pallas_call | solution.py:270

commit v6 on v4

--- a/solution.py
+++ b/solution.py
@@ -7,7 +7,7 @@
 from jax.experimental.pallas import tpu as pltpu
 from jax.sharding import PartitionSpec as P
 
-PLAN = ('F40', 'F30', 'F50', 'F60', 'F20', 'S00', 'N40', 'N50', 'N30', 'N60', 'N20', 'F41', 'F31', 'F51', 'F61', 'F21', 'S01', 'N41', 'N51', 'N31', 'N61', 'N21', 'T00', 'T40', 'T30', 'T50', 'T20', 'T60', 'T01', 'T41', 'T31', 'T51', 'T21', 'T61', 'M50', 'M30', 'M60', 'M20', 'O00', 'Y40', 'M51', 'M31', 'M61', 'M21', 'Y30', 'Y50', 'Y60', 'Y20', 'O01', 'Y41', 'Y31', 'Y51', 'L00', 'Y61', 'Y21', 'D00', 'D01', 'A60', 'A20', 'G00', 'A50', 'A30', 'A40', 'A61', 'A21', 'G01', 'A51', 'A31', 'A41', 'E00', 'E01')
+PLAN = ('F30', 'S00', 'F50', 'F60', 'F20', 'N40', 'N50', 'N30', 'N60', 'N20', 'I00', 'F40', 'F31', 'S01', 'F51', 'F61', 'F21', 'N41', 'N51', 'N31', 'N61', 'N21', 'F41', 'T00', 'T40', 'T30', 'T50', 'T20', 'T60', 'T01', 'T41', 'T31', 'T51', 'T21', 'T61', 'M50', 'M30', 'M60', 'M20', 'O00', 'H00', 'Y40', 'M51', 'M31', 'M61', 'M21', 'Y30', 'Y50', 'Y60', 'Y20', 'O01', 'Y41', 'Y31', 'Y51', 'L00', 'Y61', 'Y21', 'D00', 'D01', 'A60', 'A20', 'G00', 'A50', 'A30', 'A40', 'A61', 'A21', 'G01', 'A51', 'A31', 'A41', 'E00', 'E01')
 PARTS = 2
 MESH = pl.DeviceIdType.MESH
 NX, NY = 4, 8
@@ -23,7 +23,7 @@
     gathered, outer_out, momentum_out,
     delta, buf, side_up, side_down, near_l, near_r, far, mixed, row_out,
     to_y, from_y, outer_v, momentum_v,
-    load_sem, send_sems, recv_sems,
+    load_sem, send_sems, recv_sems, ready_sem, far_sem,
 ):
     me = lax.axis_index("rep")
     x = me // NY
@@ -47,7 +47,7 @@
     load_momentum.start()
 
     barrier = pltpu.get_barrier_semaphore()
-    partners = [right, left, across] + [place(0, dy) for dy in range(1, NY)]
+    partners = [right, left, up, down]
     for partner in partners:
         pl.semaphore_signal(barrier, inc=1, device_id={"rep": partner}, device_id_type=MESH)
 
@@ -176,6 +176,12 @@
                 x_total = x_total + wide(far.at[dy, rows])
             to_y[dy, rows] = x_total.astype(BF16)
             c["y", dy, h] = send(to_y.at[dy, rows], from_y.at[dy, rows], place(0, dy))
+        elif step == "I":
+            pl.semaphore_wait(ready_sem, len(partners))
+            for near in (2, 6):
+                pl.semaphore_signal(far_sem, inc=1, device_id={"rep": place(0, near)}, device_id_type=MESH)
+        elif step == "H":
+            pl.semaphore_wait(far_sem, 2)
         elif step == "L":
             load_outer.wait()
             load_momentum.wait()
@@ -200,6 +206,8 @@
                 c["side_down", dx, h].wait_recv()
 
     pl.semaphore_wait(barrier, len(partners))
+    for partner in partners:
+        pl.semaphore_signal(ready_sem, inc=1, device_id={"rep": partner}, device_id_type=MESH)
     for token in PLAN:
         do_step(token[0], int(token[1]), int(token[2]))
     drain()
@@ -256,6 +264,8 @@
             pltpu.SemaphoreType.DMA((NX * NY + 2,)),
             pltpu.SemaphoreType.DMA((COPIES,)),
             pltpu.SemaphoreType.DMA((COPIES,)),
+            pltpu.SemaphoreType.REGULAR,
+            pltpu.SemaphoreType.REGULAR,
         ],
         compiler_params=pltpu.CompilerParams(collective_id=0, has_side_effects=True),
         name="outer_step",

time: 37.6 us -> 36.2 us (0.963); the launches traced: 37 us -> 36 us
  Pallas kernels: 36.3 us -> 35.4 us
    pallas_call x1, Pallas kernels: 34.6 us -> 33.6 us  [shards(): pl.pallas_call(kernel, out_shape=(blocks(NX * NY), blocks(dtype=F32), blo...]
where the time goes in v6:
time: 36.2 us; the launch traced here: 36 us
  Pallas kernels  35.4 us (98%)
  between operations  0.64 us (2%)
    pallas_call x1, Pallas kernels, shards(): pl.pallas_call(kernel, out_shape=(blocks(NX * NY), blocks(dtype=F32), blo...  33.6 us
    pallas_call x1, Pallas kernels, shards(): pl.pallas_call(place_kernel, out_shape=(jax.ShapeDtypeStruct((rows, width...  1.77 us

profile of v6, /device:TPU:448, one launch (start us, length us, event | category | flops | bytes accessed | tf_op | source)
XLA Modules:
  0.0 36.0 jit_solution(8899456115512210648)
XLA Ops:
  0.6 33.6 %outer_step.1 = (bf16[32,128,128]{2,1,0:T(8,128)(2,1)S(1)}, f32[128,128]{1,0:T(8,128)S(1)}, f32[128,128]{1,0:T(8,128)S(1)}) custom-call(bf16[1,128,4096]{2,1,0:T(8,128)(2,1)} %deltas.1, s32[32]{0:T(128)} %presence.1, s32[32]{0:T(128)} %owner_of.3, f32[128,128]{1,0:T(8,128)} %outer_in.1, f32[128,128]{1,0:T(8,128)} %momentum_in.1), custom_call_target="tpu_custom_call" | custom-call | tf_op jit(solution)/shard_map/outer_step/pallas_call | solution.py:245
  34.3 1.8 %place_blocks.1 = (bf16[128,4096]{1,0:T(8,128)(2,1)}, f32[128,128]{1,0:T(8,128)}, f32[128,128]{1,0:T(8,128)}) custom-call(s32[32]{0:T(128)} %owner_of.3, bf16[32,128,128]{2,1,0:T(8,128)(2,1)S(1)} %get-tuple-element.6.gathered, f32[128,128]{1,0:T(8,128)S(1)} %get-tuple-element.7.outer_v, f32[128,128]{1,0:T(8,128)S(1)} %get-tuple-element.8.momentum_v), custom_call_target="tpu_custom_call" | custom-call | tf_op jit(solution)/shard_map/place_blocks/pallas_call | solution.py:274

commit v7 on v5

--- a/solution.py
+++ b/solution.py
@@ -35,6 +35,12 @@
     right, left = place(1, 0), place(3, 0)
     across, up, down = place(2, 0), place(0, 1), place(0, 7)
 
+    barrier = pltpu.get_barrier_semaphore()
+    near = (1, 2, 6, 7)
+    partners = [right, left, across] + [place(0, dy) for dy in near]
+    for partner in partners:
+        pl.semaphore_signal(barrier, inc=1, device_id={"rep": partner}, device_id_type=MESH)
+
     loads = [
         pltpu.make_async_copy(deltas.at[0, :, b * BLOCK : (b + 1) * BLOCK], delta.at[b], load_sem.at[b])
         for b in range(NX * NY)
@@ -45,12 +51,6 @@
     load_momentum = pltpu.make_async_copy(momentum_in, momentum_v, load_sem.at[NX * NY + 1])
     load_outer.start()
     load_momentum.start()
-
-    barrier = pltpu.get_barrier_semaphore()
-    near = (1, 2, 6, 7)
-    partners = [right, left, across] + [place(0, dy) for dy in near]
-    for partner in partners:
-        pl.semaphore_signal(barrier, inc=1, device_id={"rep": partner}, device_id_type=MESH)
 
     present = presence[me].astype(F32)
     for load in loads:

time: 36.5 us -> 36.5 us (level)
  no operation moved by 1% of the time
where the time goes in v7:
time: 36.5 us; the launch traced here: 36.3 us
  Pallas kernels  35.7 us (98%)
  between operations  0.64 us (2%)
    pallas_call x1, Pallas kernels, shards(): pl.pallas_call(kernel, out_shape=(blocks(NX * NY), blocks(dtype=F32), blo...  33.9 us
    pallas_call x1, Pallas kernels, shards(): pl.pallas_call(place_kernel, out_shape=(jax.ShapeDtypeStruct((rows, width...  1.77 us

profile of v7, /device:TPU:448, one launch (start us, length us, event | category | flops | bytes accessed | tf_op | source)
XLA Modules:
  0.0 36.3 jit_solution(14551621960084143684)
XLA Ops:
  0.6 33.9 %outer_step.1 = (bf16[32,128,128]{2,1,0:T(8,128)(2,1)S(1)}, f32[128,128]{1,0:T(8,128)S(1)}, f32[128,128]{1,0:T(8,128)S(1)}) custom-call(bf16[1,128,4096]{2,1,0:T(8,128)(2,1)} %deltas.1, s32[32]{0:T(128)} %presence.1, s32[32]{0:T(128)} %owner_of.3, f32[128,128]{1,0:T(8,128)} %outer_in.1, f32[128,128]{1,0:T(8,128)} %momentum_in.1), custom_call_target="tpu_custom_call" | custom-call | tf_op jit(solution)/shard_map/outer_step/pallas_call | solution.py:242
  34.5 1.8 %place_blocks.1 = (bf16[128,4096]{1,0:T(8,128)(2,1)}, f32[128,128]{1,0:T(8,128)}, f32[128,128]{1,0:T(8,128)}) custom-call(s32[32]{0:T(128)} %owner_of.3, bf16[32,128,128]{2,1,0:T(8,128)(2,1)S(1)} %get-tuple-element.6.gathered, f32[128,128]{1,0:T(8,128)S(1)} %get-tuple-element.7.outer_v, f32[128,128]{1,0:T(8,128)S(1)} %get-tuple-element.8.momentum_v), custom_call_target="tpu_custom_call" | custom-call | tf_op jit(solution)/shard_map/place_blocks/pallas_call | solution.py:270
